TPU v7x, 512 devices: a whole 4x8x8 slice. The times are simulated.
512 devices in a mesh: band: 2 (over core), tmpl: 32 (over z, x), tm: 8 (over y).
Axes of the slice: x: 4, y: 8, z: 8, core: 2. Of those that a mesh axis runs over, the one named last changes fastest.
Arguments:
- strain_high: float32 [65536], P('tm'), may hold values from -6 to 6
- strain_mid: float32 [8192], P('tm'), may hold values from -6 to 6
- strain_low: float32 [1024], P('tm'), may hold values from -6 to 6
- filters_high: float32 [320, 1024], P('tmpl'), may hold values from -0.1875 to 0.1875
- filters_mid: float32 [320, 1024], P('tmpl'), may hold values from -0.1875 to 0.1875
- filters_low: float32 [320, 128], P('tmpl'), may hold values from -0.5 to 0.5
- recon_high: float32 [320, 2, 2048], P(None, None, 'tmpl'), may hold values from -0.3125 to 0.3125
- recon_mid: float32 [320, 2, 2048], P(None, None, 'tmpl'), may hold values from -0.3125 to 0.3125
- recon_low: float32 [320, 2, 2048], P(None, None, 'tmpl'), may hold values from -0.3125 to 0.3125
- basis_count: int32 [3], replicated, may hold values from 160 to 320
Outputs:
- snr: float32 [2, 2048, 65536], P('band', 'tmpl', 'tm')
Inputs may be any that keep to these rules, and one draw needn't show every extreme that they name: basis_count[b] says how many of the first 320 basis vectors band b uses.
All inputs are finite; a program needn't handle non-finite values.
Results may differ from a plain program's by a relative error of at most 0.000082.
Values sent between devices are 32-bit elements; how exact they have to be, the bound alone decides.
No kernel may reach another device: no remote copies, remote signals or barrier semaphores. Data moves between devices by JAX's collectives and lax.ppermute only.
A program may use at most 128 MiB of HBM per device.

v0:
```python
import functools

import jax
import jax.numpy as jnp
import numpy as np
from jax import lax
from jax.experimental import pallas as pl
from jax.experimental.pallas import tpu as pltpu
from jax.sharding import PartitionSpec as P


RATIO = 8
HALF_TAPS = 8
LANES = 128
ROWS = 8
SHARES = 4
BF16 = jnp.bfloat16
F32 = jnp.float32


def interp_blocks():
    phase = np.arange(RATIO)[:, None] / RATIO
    lag = np.arange(2 * HALF_TAPS)[None, :]
    v = phase - (lag - HALF_TAPS)
    g = np.sinc(v) * (0.5 + 0.5 * np.cos(np.pi * v / (HALF_TAPS + 1)))
    blocks = np.zeros((4, 256, 256), np.float64)
    for r in range(4):
        for n in range(256):
            for q in range(2 * HALF_TAPS):
                blocks[r, 32 * r + n // RATIO + q, n] = g[n % RATIO, q]
    return blocks


def split(x):
    hi = x.astype(BF16)
    lo = (x - hi.astype(F32)).astype(BF16)
    return hi, lo


def dot(a, b):
    return lax.dot_general(a, b, (((1,), (0,)), ((), ())), preferred_element_type=F32)


def dot3(a_hi, a_lo, b_hi, b_lo):
    left = jnp.concatenate([a_hi, a_lo, a_hi], axis=1)
    right = jnp.concatenate([b_hi, b_hi, b_lo], axis=0)
    return dot(left, right)


def rebuild(hi, lo, up_hi_ref, up_lo_ref, r):
    if r == 3:
        return dot3(hi, lo, up_hi_ref[r], up_lo_ref[r])
    first_hi, first_lo = hi[:, :LANES], lo[:, :LANES]
    return dot3(first_hi, first_lo, up_hi_ref[r, :LANES, :], up_lo_ref[r, :LANES, :])


def lane_iota(rows):
    return lax.broadcasted_iota(jnp.int32, (rows, LANES), 1)


def pack_filters(
    place, count_ref, high_ref, mid_ref, low_ref, rhigh_ref, rmid_ref, rlow_ref, shigh_ref, smid_ref, slow_ref,
    out_ref, w_hi_ref, w_lo_ref, l_hi_ref, l_lo_ref, strain_ref, edge_ref, line_ref,
):
    band, slot = place()
    share = slot % SHARES
    rows = high_ref.shape[0]
    for t in range(2):
        start = pl.multiple_of(share * 256 + t * LANES, LANES)
        high = high_ref[:, pl.ds(start, LANES)]
        mid = mid_ref[:, pl.ds(start, LANES)]
        line_ref[rows * t : rows * (t + 1), :] = jnp.where(band == 0, high, mid)
    low = pltpu.roll(low_ref[...], (LANES - 32 * share) % LANES, 1)
    turned = [low] + [pltpu.roll(low, 32 * k, 1) for k in (1, 2, 3)]
    lane = lane_iota(1)
    for first in range(0, 12, 4):
        value = jnp.zeros((1, LANES), F32)
        for q in range(first, min(first + 4, rows)):
            at = 32 * (q - first)
            value = jnp.where((lane >= at) & (lane < at + 32), turned[q - first][q : q + 1, :], value)
        line_ref[2 * rows + first // 4 : 2 * rows + first // 4 + 1, :] = value
    line_ref[2 * rows + 3 : 24, :] = jnp.zeros((24 - 2 * rows - 3, LANES), F32)
    line = line_ref[...]
    for p in range(out_ref.shape[0]):
        out_ref[p] = line
    strain_ref[0:64, :] = shigh_ref[...]
    edge_ref[0:8, :] = shigh_ref[56:64, :]
    edge_ref[8:16, :] = smid_ref[...]
    edge_ref[16:24, :] = jnp.broadcast_to(slow_ref[...], (ROWS, LANES))
    column = lax.broadcasted_iota(jnp.int32, rhigh_ref.shape, 1)
    limit = jnp.where(band == 0, count_ref[0], count_ref[1])
    weights = jnp.where(column < limit, jnp.where(band == 0, rhigh_ref[...], rmid_ref[...]), 0.0)
    w_hi_ref[...], w_lo_ref[...] = split(weights)
    l_hi_ref[...], l_lo_ref[...] = split(jnp.where(column < count_ref[2], rlow_ref[...], 0.0))


def combine(place, got_ref, w_hi_ref, w_lo_ref, l_hi_ref, l_lo_ref, edge_ref, out_ref, f_ref):
    band, _ = place()
    parts = got_ref.shape[0]
    basis = w_hi_ref.shape[1]
    rows = basis // parts
    for q in range(rows):
        at = pl.ds(q, parts, stride=rows)
        for t in range(2):
            f_ref[t, at, :] = got_ref[:, rows * t + q, :]
        low = got_ref[:, 2 * rows + q // 4, :]
        f_ref[2, at, :] = pltpu.roll(low, LANES - 32 * (q % 4), 1) if q % 4 else low
    taps = jnp.concatenate([f_ref[t] for t in range(2)], axis=1)
    h = dot3(w_hi_ref[...], w_lo_ref[...], *split(taps))
    wide = h.shape[0]
    out_ref[0:wide, :] = h[:, :LANES]
    out_ref[wide : 2 * wide, :] = h[:, LANES:]
    low = jnp.transpose(dot3(l_hi_ref[...], l_lo_ref[...], *split(f_ref[2])))[0:32, :]
    edge = jnp.concatenate([edge_ref[...], jnp.zeros((ROWS, LANES), F32)], axis=0)
    out_ref[2 * wide : 2 * wide + 32, :] = jnp.where(band == 0, edge, low)


def select(place, both_ref, out_ref):
    band, _ = place()
    size = both_ref.shape[0] // 2
    tmpl = (size - 32) // 4
    for k in range(4):
        start = size * (k // 2) + 2 * tmpl * (k % 2) + band * tmpl
        out_ref[k * tmpl : (k + 1) * tmpl, :] = both_ref[pl.ds(pl.multiple_of(start, tmpl), tmpl), :]
    low = both_ref[size + 4 * tmpl :, :]
    low = jnp.where(band == 0, low, pltpu.roll(low, 64, 1))
    tail = both_ref[4 * tmpl : 4 * tmpl + 8, :]
    mid = both_ref[4 * tmpl + 8 : 4 * tmpl + 16, :]
    strain = jnp.concatenate([pltpu.roll(tail, 64, 1), tail, pltpu.roll(mid, 64, 1), mid], axis=0)
    out_ref[4 * tmpl : 4 * tmpl + 32, :] = jnp.where(lane_iota(32) < 64, low, strain)
    out_ref[4 * tmpl + 32 :, :] = both_ref[4 * tmpl + 16 : 4 * tmpl + 24, :]


class Toeplitz:
    def __init__(self, source, shift, hi_ref, lo_ref):
        self.source, self.shift, self.hi_ref, self.lo_ref = source, shift, hi_ref, lo_ref
        self.turned = {}
        self.lane = lane_iota(ROWS)
        self.sub = lax.broadcasted_iota(jnp.int32, (ROWS, LANES), 0)

    def turn(self, group, n):
        key = (group, n)
        if key not in self.turned:
            by = (ROWS * group + self.shift) % LANES
            self.turned[key] = pltpu.roll(self.source(n), by, 1, stride=1, stride_axis=0)
        return self.turned[key]

    def eight(self, group, n):
        by = ROWS * group + self.shift
        amount = self.sub + by
        value = jnp.where(self.lane >= amount, self.turn(group, n), self.turn(group, n - 1))
        if by + ROWS - 1 > LANES:
            value = jnp.where(self.lane >= amount - LANES, value, self.turn(group, n - 2))
        return value

    def build(self, n, column):
        for pair in range(LANES // 16):
            value = jnp.concatenate([self.eight(2 * pair, n), self.eight(2 * pair + 1, n)], axis=0)
            hi, lo = split(value)
            at = (pl.ds(16 * pair, 16), pl.ds(LANES * column, LANES))
            self.hi_ref[at] = hi
            self.lo_ref[at] = lo


def wide(hi_ref, lo_ref, start, width):
    def pair(ref):
        return [ref[:, start : start + width], ref[:, start - LANES : start - LANES + width]]

    return jnp.concatenate(pair(hi_ref) + pair(hi_ref) + pair(lo_ref), axis=0)


def narrow(hi, lo, t_hi, t_lo, start):
    two = [jnp.concatenate([r[:, start : start + 256], r[:, start - LANES : start + LANES]], axis=0) for r in (t_hi, t_lo)]
    count = hi.shape[0]
    first = dot(jnp.concatenate([hi, lo], axis=0), two[0])
    return first[:count] + first[count:] + dot(hi, two[1])


def rows_of(ref):
    return lambda n: jnp.broadcast_to(ref[n : n + 1, :], (ROWS, LANES))


def filter_own(own_ref, strain_ref, t_hi, t_lo, out_ref):
    tmpl = out_ref.shape[0]
    blocks = out_ref.shape[1] // 256 - 3
    own = Toeplitz(lambda n: jnp.broadcast_to(strain_ref[n - 8 : n - 7, :], (ROWS, LANES)), 0, t_hi, t_lo)
    hi, lo = split(jnp.concatenate([own_ref[0:tmpl, :], own_ref[tmpl : 2 * tmpl, :]], axis=1))
    both = jnp.concatenate([hi, lo], axis=0)
    out_ref[:, 0 : 4 * 256] = jnp.zeros((tmpl, 4 * 256), F32)
    own.build(9, 9)
    for m in range(1, blocks):
        own.build(2 * m + 8, 2 * m + 8)
        own.build(2 * m + 9, 2 * m + 9)
        start = 256 * m + 1024
        taps = [jnp.concatenate([r[:, start : start + 256], r[:, start - LANES : start + LANES]], axis=0) for r in (t_hi, t_lo)]
        first = dot(both, taps[0])
        out_ref[:, 256 * (m + 3) : 256 * (m + 4)] = first[:tmpl] + first[tmpl:] + dot(hi, taps[1])


def column(block):
    return pl.ds(pl.multiple_of(256 * block, 256), 256)


def filter_two(place, right_ref, second_ref, t_hi, t_lo, done_ref, out_ref, b1_ref, b2_ref):
    _, slot = place()
    tmpl = out_ref.shape[0]
    blocks = out_ref.shape[1] // 256
    taps = [jnp.concatenate([r[0:tmpl, :], r[tmpl : 2 * tmpl, :]], axis=1) for r in (right_ref, second_ref)]
    hi, lo = split(jnp.concatenate(taps, axis=0))
    for ref in (b1_ref, b2_ref):
        ref[:, 0 : 4 * 256] = jnp.zeros((tmpl, 4 * 256), F32)
    for m in range(1, blocks):
        got = narrow(hi, lo, t_hi, t_lo, 256 * m + 1024)
        b1_ref[:, 256 * (m + 3) : 256 * (m + 4)] = got[:tmpl]
        b2_ref[:, 256 * (m + 3) : 256 * (m + 4)] = got[tmpl:]
        at = [column(m + 3 - (slot + ahead) % SHARES) for ahead in range(3)]
        out_ref[:, 256 * m : 256 * m + 256] = done_ref[:, at[0]] + b1_ref[:, at[1]] + b2_ref[:, at[2]]


def filter_and_rebuild(
    place, own_ref, left_ref, right_ref, second_ref, strain_ref, t_hi, t_lo, part_ref, up_hi_ref, up_lo_ref, result_ref,
    out_ref, head_ref, z0_ref, z1_ref, z2_ref, b3_ref, sem_ref, xh_ref, ym_ref, yl_ref, th_hi, th_lo, tm_hi, tm_lo, tl_hi, tl_lo, hh_ref, hm_ref, sm_ref,
    hl_ref, hc_ref,
):
    _, slot, slots = place()
    tmpl = out_ref.shape[0]
    base = 4 * tmpl
    lane = lane_iota(ROWS)

    def edges(ref, keep):
        def wide(first):
            a, b = ref[first : first + 8, :], ref[first + 8 : first + 16, :]
            return jnp.where(keep, jnp.where(lane < 64, pltpu.roll(a, 64, 1), b), 0.0)

        return wide(base), wide(base + 16), jnp.where(keep, ref[base + 32 : base + 40, :], 0.0)

    here = edges(own_ref, slot >= 0)
    left = edges(left_ref, slot >= 1)
    second = edges(second_ref, slot >= 2)
    right = edges(right_ref, slot < slots - 1)
    xh_ref[0:8, :] = left[0]
    xh_ref[8:16, :] = strain_ref[0:8, :]
    for k, block in enumerate((second, left, here, right)):
        ym_ref[8 * k : 8 * k + 8, :] = block[1]
        yl_ref[k : k + 1, :] = block[2][0:1, :]

    for source, ahead in ((own_ref, 0), (right_ref, 1), (second_ref, 2), (left_ref, 3)):
        share = (slot + ahead) % SHARES
        for k in range(4):
            hi, lo = split(source[k * tmpl : (k + 1) * tmpl, :])
            ref, at = (hh_ref, hm_ref)[k // 2], LANES * (k % 2)
            rows = pl.ds(pl.multiple_of(share * tmpl, tmpl), tmpl) if k // 2 else slice(ahead * tmpl, (ahead + 1) * tmpl)
            places = [(ref, rows)]
            if k // 2 == 0:
                places.append((hc_ref, pl.ds(pl.multiple_of(share * tmpl, tmpl), tmpl)))
            for ref, rows in places:
                ref[rows, at : at + LANES] = hi
                ref[rows, 256 + at : 256 + at + LANES] = lo
                ref[rows, 512 + at : 512 + at + LANES] = hi
        hl_ref[pl.ds(pl.multiple_of(share * 32, 32), 32), :] = source[base : base + 32, :]
    h_low = jnp.transpose(hl_ref[...])[0:tmpl, :]

    blocks = out_ref.shape[1] // 256
    copies, sent = [], 0
    zero_block = (z0_ref, z1_ref, z2_ref, b3_ref)
    shares = [(slot + ahead) % SHARES for ahead in range(SHARES)]
    high_t = Toeplitz(rows_of(xh_ref), 0, th_hi, th_lo)
    mid_t = Toeplitz(rows_of(ym_ref), 8, tm_hi, tm_lo)
    low_t = Toeplitz(rows_of(yl_ref), 9, tl_hi, tl_lo)

    def columns(m):
        return slice(256 * m, 256 * m + 256)

    head_ref[...] = jnp.zeros(head_ref.shape, F32)

    def inner(m):
        if m == 0:
            got = dot(hh_ref[...], wide(th_hi, th_lo, 1024, 256))
            for ahead, ref in enumerate(zero_block):
                ref[:, columns(3)] = got[ahead * tmpl : (ahead + 1) * tmpl, :]
            return
        hi, lo = hh_ref[3 * tmpl :, 0:256], hh_ref[3 * tmpl :, 256:512]
        b3_ref[:, columns(m + 3)] = narrow(hi, lo, t_hi, t_lo, 256 * m + 1024)

    def outer(m):
        got = dot(hc_ref[-m * tmpl :, :], wide(th_hi, th_lo, 256 * m + 1024, 256))
        for k in range(SHARES + m):
            head_ref[:, columns(k)] += got[k * tmpl : (k + 1) * tmpl, :]

    def finish(a):
        value = out_ref[:, columns(a)] + b3_ref[:, column(a + 3 - shares[3])]
        if a > 0:
            value = value + part_ref[:, columns(a)]
        if a < SHARES:
            for ahead in range(3):
                value = value + zero_block[ahead][:, column(a + 3 - shares[ahead])]
        if a < 3:
            value = value + head_ref[:, columns(a)]
        out_ref[:, columns(a)] = value

    def send(first, last):
        where = (slice(None), pl.ds(256 * first, 256 * (last - first)))
        copy = pltpu.make_async_copy(out_ref.at[where], result_ref.at[where], sem_ref.at[len(copies)])
        copy.start()
        copies.append(copy)

    for n in range(1, 10):
        high_t.build(n, n)
    for m in (-3, -2, -1):
        outer(m)
    for m in range(0, 8):
        inner(m)
        mid_t.build(2 * m + 9, 2 * m + 1)
        mid_t.build(2 * m + 10, 2 * m + 2)

    low_t.build(2, 0)
    low_t.build(3, 1)
    part_low = dot3(*split(h_low), tl_hi[...], tl_lo[...])
    low_count = LANES
    z = lax.broadcasted_iota(jnp.int32, part_low.shape, 1) - 9 + slot * low_count
    part_low = jnp.where((z >= 0) & (z < slots * low_count), part_low, 0.0)
    low_hi, low_lo = split(part_low)

    edge = jnp.zeros((tmpl, LANES), F32)
    for c in range(4):
        edge = edge + dot(hm_ref[c * tmpl : (c + 1) * tmpl, :], wide(tm_hi, tm_lo, 2048 - 256 * c, LANES))
    for r in range(4):
        sm_ref[:, 256 * r : 256 * r + 256] = rebuild(low_hi, low_lo, up_hi_ref, up_lo_ref, r)
    sm_ref[:, 1024:1152] = edge + dot3(
        low_hi[:, LANES:], low_lo[:, LANES:], up_hi_ref[0, 0:LANES, 0:LANES], up_lo_ref[0, 0:LANES, 0:LANES]
    )
    for m in range(-3, 4):
        first, last = max(0, -m), min(3, 3 - m)
        got = dot(hm_ref[first * tmpl : (last + 1) * tmpl, :], wide(tm_hi, tm_lo, 256 * m + 1024, 256))
        for c in range(first, last + 1):
            at = 256 * (m + c)
            sm_ref[:, at : at + 256] += got[(c - first) * tmpl : (c - first + 1) * tmpl, :]
    for ref in zero_block[:3]:
        ref[:, 0:768] = jnp.zeros((tmpl, 768), F32)
        ref[:, 1024:] = jnp.zeros((tmpl, 768), F32)
    b3_ref[:, 0:768] = jnp.zeros((tmpl, 768), F32)
    inner(8)
    inner(9)
    mid_count = 1024
    v = lax.broadcasted_iota(jnp.int32, sm_ref.shape, 1) - 8 + slot * mid_count
    part_mid = jnp.where((v >= 0) & (v < slots * mid_count), sm_ref[...], 0.0)
    mid_hi, mid_lo = split(part_mid)

    def stacked(x):
        return jnp.concatenate([x[:, LANES * g : LANES * g + 256] for g in range(8)], axis=0)

    stack_hi, stack_lo = stacked(mid_hi), stacked(mid_lo)
    for r in range(4):
        got = rebuild(stack_hi, stack_lo, up_hi_ref, up_lo_ref, r)
        for g in range(8):
            out_ref[:, columns(4 * g + r)] = got[g * tmpl : (g + 1) * tmpl, :]
    ready = 10
    for m in range(ready, blocks):
        inner(m)
        if m == ready:
            for a in range(m + 1):
                finish(a)
        else:
            finish(m)
        if m % 4 == 3 or m >= blocks - 2:
            send(sent, m + 1)
            sent = m + 1
    for copy in copies:
        copy.wait()


VMEM = pl.BlockSpec(memory_space=pltpu.VMEM)
SMEM = pl.BlockSpec(memory_space=pltpu.SMEM)
ANY = pl.BlockSpec(memory_space=pl.ANY)


def near(x):
    return pltpu.with_memory_space_constraint(x, pltpu.VMEM)


def place():
    return lax.axis_index("band").astype(jnp.int32), lax.axis_index("tm").astype(jnp.int32)


def call_pack(count, filters, recons, strains, parts, place=place):
    wide, basis = recons[0].shape
    half = pltpu.VMEM((wide, basis), BF16)
    return pl.pallas_call(
        functools.partial(pack_filters, place),
        out_shape=(
            pltpu.VMEM((parts, 24, LANES), F32), half, half, half, half,
            pltpu.VMEM(strains[0].shape, F32), pltpu.VMEM((24, LANES), F32),
        ),
        in_specs=[SMEM] + [VMEM] * 9,
        out_specs=(VMEM,) * 7,
        scratch_shapes=[pltpu.VMEM((24, LANES), F32)],
        name="pack_filters",
    )(count, *filters, *recons, *strains)


def call_combine(got, weights, edge, place=place):
    wide, basis = weights[0].shape
    return pl.pallas_call(
        functools.partial(combine, place),
        out_shape=pltpu.VMEM((2 * wide + 32, LANES), F32),
        in_specs=[VMEM] * 6,
        out_specs=VMEM,
        scratch_shapes=[pltpu.VMEM((3, basis, LANES), F32)],
        name="combine",
    )(*[near(x) for x in (got, *weights, edge)])


def call_select(both, place=place):
    return pl.pallas_call(
        functools.partial(select, place),
        out_shape=pltpu.VMEM((both.shape[0] // 2 + 8, LANES), F32),
        in_specs=[VMEM],
        out_specs=VMEM,
        name="select",
    )(near(both))


def call_filter_own(own, strain, tmpl, count):
    half = pltpu.VMEM((LANES, count + 1024), BF16)
    return pl.pallas_call(
        filter_own,
        out_shape=(half, half, pltpu.VMEM((tmpl, count + 768), F32)),
        in_specs=[VMEM] * 2,
        out_specs=(VMEM,) * 3,
        name="filter_own",
        compiler_params=pltpu.CompilerParams(vmem_limit_bytes=24 << 20),
    )(near(own), near(strain))


def call_filter_two(right, second, t_hi, t_lo, done, tmpl, count, place=place):
    return pl.pallas_call(
        functools.partial(filter_two, place),
        out_shape=pltpu.VMEM((tmpl, count), F32),
        in_specs=[VMEM] * 5,
        out_specs=VMEM,
        scratch_shapes=[pltpu.VMEM((tmpl, count + 768), F32)] * 2,
        name="filter_two",
        compiler_params=pltpu.CompilerParams(vmem_limit_bytes=24 << 20),
    )(*[near(x) for x in (right, second, t_hi, t_lo, done)])


def call_filter(own, left, right, second, strain, t_hi, t_lo, part, up_hi, up_lo, tmpl, count, slots, place=place):
    return pl.pallas_call(
        functools.partial(filter_and_rebuild, lambda: (*place(), slots)),
        out_shape=jax.ShapeDtypeStruct((tmpl, count), F32),
        in_specs=[VMEM] * 10,
        out_specs=ANY,
        scratch_shapes=[
            pltpu.VMEM((tmpl, count), F32),
            pltpu.VMEM((tmpl, 768), F32),
            pltpu.VMEM((tmpl, 7 * 256), F32),
            pltpu.VMEM((tmpl, 7 * 256), F32),
            pltpu.VMEM((tmpl, 7 * 256), F32),
            pltpu.VMEM((tmpl, count + 768), F32),
            pltpu.SemaphoreType.DMA((count // 1024 + 1,)),
            pltpu.VMEM((16, LANES), F32),
            pltpu.VMEM((32, LANES), F32),
            pltpu.VMEM((8, LANES), F32),
            pltpu.VMEM((LANES, 1280), BF16),
            pltpu.VMEM((LANES, 1280), BF16),
            pltpu.VMEM((LANES, 2304), BF16),
            pltpu.VMEM((LANES, 2304), BF16),
            pltpu.VMEM((LANES, 256), BF16),
            pltpu.VMEM((LANES, 256), BF16),
            pltpu.VMEM((4 * tmpl, 768), BF16),
            pltpu.VMEM((4 * tmpl, 768), BF16),
            pltpu.VMEM((tmpl, 1152), F32),
            pltpu.VMEM((LANES, LANES), F32),
            pltpu.VMEM((4 * tmpl, 768), BF16),
        ],
        name="filter_and_rebuild",
        compiler_params=pltpu.CompilerParams(vmem_limit_bytes=36 << 20),
    )(*[near(x) for x in (own, left, right, second, strain, t_hi, t_lo, part, up_hi, up_lo)])


def interp_halves():
    exact = jnp.asarray(interp_blocks().astype(np.float32))
    return split(exact)


def local(
    strain_high, strain_mid, strain_low,
    filters_high, filters_mid, filters_low,
    recon_high, recon_mid, recon_low, basis_count,
):
    tmpl_count = lax.axis_size("tmpl")

    def turned(recon):
        basis, parts, count = recon.shape
        return jnp.transpose(recon, (1, 2, 0)).reshape(parts * count, basis)

    packed, *weights, strain, edge = call_pack(
        basis_count,
        (filters_high, filters_mid, filters_low),
        (turned(recon_high), turned(recon_mid), turned(recon_low)),
        (strain_high.reshape(-1, LANES), strain_mid.reshape(-1, LANES), strain_low.reshape(1, LANES)),
        tmpl_count,
    )
    slots = lax.axis_size("tm")
    got = lax.all_to_all(packed, "tmpl", 0, 0, tiled=True)
    both = lax.all_gather(call_combine(got, weights, edge), "band", axis=0, tiled=True)
    own = call_select(both)

    def moved(by):
        return lax.ppermute(own, "tm", [(i, (i + by) % slots) for i in range(slots)])

    second, right, left = moved(2), moved(-1), moved(1)
    tmpl, count = recon_high.shape[2], strain_high.shape[0]
    t_hi, t_lo, done = call_filter_own(own, strain, tmpl, count)
    begun = (t_hi, t_lo, call_filter_two(right, second, t_hi, t_lo, done, tmpl, count))
    up_hi, up_lo = interp_halves()
    out = call_filter(own, left, right, second, strain, *begun, up_hi, up_lo, tmpl, count, slots)
    return out[None]


def solution(mesh):
    in_specs = (
        P("tm"), P("tm"), P("tm"),
        P("tmpl", None), P("tmpl", None), P("tmpl", None),
        P(None, None, "tmpl"), P(None, None, "tmpl"), P(None, None, "tmpl"),
        P(),
    )
    out_specs = P("band", "tmpl", "tm")
    return jax.shard_map(local, mesh=mesh, in_specs=in_specs, out_specs=out_specs, check_vma=False)
```

profile of v0, /device:TPU:1, one launch (start us, length us, event | category | flops | bytes accessed | tf_op | source)
XLA Modules:
  0.0 57.2 jit_solution(1535156070255497793)
XLA Ops:
  0.0 1.4 %pack_filters.1 = (f32[32,24,128]{2,1,0:T(8,128)S(1)}, bf16[128,320]{1,0:T(8,128)(2,1)S(1)}, bf16[128,320]{1,0:T(8,128)(2,1)S(1)}, bf16[128,320]{1,0:T(8,128)(2,...) custom-call(s32[3]{0:T(128)} %count_ref.1, f32[10,1024]{1,0:T(8,128)} %high_ref.1, ...), custom_call_target="tpu_custom_call" | custom-call | tf_op jit(solution)/shard_map/pack_filters/pallas_call | solution.py:388
  1.4 27.3 %all_to_all.5.got_ref = f32[32,24,128]{2,1,0:T(8,128)S(1)} all-to-all(f32[32,24,128]{2,1,0:T(8,128)S(1)} %get-tuple-element.15), channel_id=1, replica_groups=mesh['band'=2,'tmpl'=32,'tm'=8] {'tmpl'}, dimensions={0} | all-to-all | bytes 786432 | tf_op jit(solution)/shard_map/all_to_all | solution.py:505
  28.8 0.6 %combine.1 = f32[288,128]{1,0:T(8,128)S(1)} custom-call(f32[32,24,128]{2,1,0:T(8,128)S(1)} %all_to_all.5.got_ref, bf16[128,320]{1,0:T(8,128)(2,1)S(1)} %get-tuple-element.16.w_hi_ref, bf16[128,320]{1,0:T(8,128)(2,1)S(1)} %get-tuple-element.17.w_lo_ref, bf16[128,320]{1,0:T(8,128)(2,1)S(1)} %get-tuple-element.18.l_hi_ref, ...), custom_call_target="tpu_custom_call" | custom-call | tf_op jit(solution)/shard_map/combine/pallas_call | solution.py:403
  29.4 4.1 %all_gather.3.both_ref = f32[576,128]{1,0:T(8,128)S(1)} all-gather(f32[288,128]{1,0:T(8,128)S(1)} %combine.1), channel_id=1, replica_groups=mesh['band'=2,'tmpl'=32,'tm'=8] {'band'}, dimensions={0}, use_global_device_ids=true | all-gather | bytes 442368 | tf_op jit(solution)/shard_map/all_gather | solution.py:506
  33.4 0.1 select.1.own_ref
  33.5 5.1 %collective-permute-start.1 = (f32[296,128]{1,0:T(8,128)S(1)}, f32[296,128]{1,0:T(8,128)S(1)}, u32[]{:S(2)}, u32[]{:S(2)}) collective-permute-start(f32[296,128]{1,0:T(8,128)S(1)} %select.1.own_ref), channel_id=1, source_target_pairs={{0,7},{1,0},{2,1},{3,2},{4,3},{5,4},{6,5},{7,6},{8,15},{9,8},{10,9... | collective-permute-start | bytes 454664 | tf_op jit(solution)/shard_map/ppermute | solution.py:510
  38.6 1.9 %collective-permute-start.2 = (f32[296,128]{1,0:T(8,128)S(1)}, f32[296,128]{1,0:T(8,128)S(1)}, u32[]{:S(2)}, u32[]{:S(2)}) collective-permute-start(f32[296,128]{1,0:T(8,128)S(1)} %select.1.own_ref), channel_id=1, source_target_pairs={{0,2},{1,3},{2,4},{3,5},{4,6},{5,7},{6,0},{7,1},{8,10},{9,11},{10,... | collective-permute-start | bytes 454664 | tf_op jit(solution)/shard_map/ppermute | solution.py:510
  40.5 2.5 %collective-permute-start = (f32[296,128]{1,0:T(8,128)S(1)}, f32[296,128]{1,0:T(8,128)S(1)}, u32[]{:S(2)}, u32[]{:S(2)}) collective-permute-start(f32[296,128]{1,0:T(8,128)S(1)} %select.1.own_ref), channel_id=1, source_target_pairs={{0,1},{1,2},{2,3},{3,4},{4,5},{5,6},{6,7},{7,0},{8,9},{9,10},{10,1... | collective-permute-start | bytes 454664 | tf_op jit(solution)/shard_map/ppermute | solution.py:510
  43.0 2.0 %filter_own.1 = (bf16[128,9216]{1,0:T(8,128)(2,1)S(1)}, bf16[128,9216]{1,0:T(8,128)(2,1)S(1)}, f32[64,8960]{1,0:T(8,128)S(1)}) custom-call(f32[296,128]{1,0:T(8,128)S(1)} %select.1.own_ref, f32[64,128]{1,0:T(8,128)S(1)} %get-tuple-element.21.strain_ref), custom_call_target="tpu_custom_call" | custom-call | tf_op jit(solution)/shard_map/filter_own/pallas_call | solution.py:425
  45.0 0.0 collective-permute-done.1.right_ref
  45.0 5.2 %collective-permute-done.2.second_ref = f32[296,128]{1,0:T(8,128)S(1)} collective-permute-done((f32[296,128]{1,0:T(8,128)S(1)}, f32[296,128]{1,0:T(8,128)S(1)}, u32[]{:S(2)}, u32[]{:S(2)}) %collective-permute-start.2) | collective-permute-done | bytes 151584 | tf_op jit(solution)/shard_map/ppermute | solution.py:510
  50.2 0.0 copy-start
  50.2 0.0 copy-start.1
  50.2 2.1 %filter_two.1.part_ref = f32[64,8192]{1,0:T(8,128)S(1)} custom-call(f32[296,128]{1,0:T(8,128)S(1)} %collective-permute-done.1.right_ref, f32[296,128]{1,0:T(8,128)S(1)} %collective-permute-done.2.second_ref, bf16[128,9216]{1,0:T(8,128)(2,1)S(1)} %get-tuple-element.22.t_hi, bf16[128,9216]{1,0:T(8,128)(2,1)S(1)} %get-tuple-element.23.t_lo, ...), custom_call_target="tpu_custom_call" | custom-call | tf_op jit(solution)/shard_map/filter_two/pallas_call | solution.py:436
  52.3 0.1 collective-permute-done.left_ref
  52.4 0.0 copy-done
  52.4 0.0 copy-done.1
  52.4 4.8 %filter_and_rebuild.1 = f32[64,8192]{1,0:T(8,128)} custom-call(f32[296,128]{1,0:T(8,128)S(1)} %select.1.own_ref, f32[296,128]{1,0:T(8,128)S(1)} %collective-permute-done.left_ref, f32[296,128]{1,0:T(8,128)S(1)} %collective-permute-done.1.right_ref, f32[296,128]{1,0:T(8,128)S(1)} %collective-permute-done.2.second_ref, ...), custom_call_target="tpu_custom_call" | custom-call | tf_op jit(solution)/shard_map/filter_and_rebuild/pallas_call | solution.py:448
Async XLA Ops:
  33.5 11.5 %collective-permute-start.1 = (f32[296,128]{1,0:T(8,128)S(1)}, f32[296,128]{1,0:T(8,128)S(1)}, u32[]{:S(2)}, u32[]{:S(2)}) collective-permute-start(f32[296,128]{1,0:T(8,128)S(1)} %select.1.own_ref), channel_id=1, source_target_pairs={{0,7},{1,0},{2,1},{3,2},{4,3},{5,4},{6,5},{7,6},{8,15},{9,8},{10,9... | collective-permute-start | bytes 454664 | tf_op jit(solution)/shard_map/ppermute | solution.py:510
  38.6 11.6 %collective-permute-start.2 = (f32[296,128]{1,0:T(8,128)S(1)}, f32[296,128]{1,0:T(8,128)S(1)}, u32[]{:S(2)}, u32[]{:S(2)}) collective-permute-start(f32[296,128]{1,0:T(8,128)S(1)} %select.1.own_ref), channel_id=1, source_target_pairs={{0,2},{1,3},{2,4},{3,5},{4,6},{5,7},{6,0},{7,1},{8,10},{9,11},{10,... | collective-permute-start | bytes 454664 | tf_op jit(solution)/shard_map/ppermute | solution.py:510
  40.5 11.8 %collective-permute-start = (f32[296,128]{1,0:T(8,128)S(1)}, f32[296,128]{1,0:T(8,128)S(1)}, u32[]{:S(2)}, u32[]{:S(2)}) collective-permute-start(f32[296,128]{1,0:T(8,128)S(1)} %select.1.own_ref), channel_id=1, source_target_pairs={{0,1},{1,2},{2,3},{3,4},{4,5},{5,6},{6,7},{7,0},{8,9},{9,10},{10,1... | collective-permute-start | bytes 454664 | tf_op jit(solution)/shard_map/ppermute | solution.py:510
  50.2 2.2 %copy-start = (bf16[4,256,256]{2,1,0:T(8,128)(2,1)S(1)}, bf16[4,256,256]{2,1,0:T(8,128)(2,1)}, u32[]{:S(2)}) copy-start(bf16[4,256,256]{2,1,0:T(8,128)(2,1)} %constant.6.up_hi_ref) | copy-start | bytes 1572868
  50.2 2.2 %copy-start.1 = (bf16[4,256,256]{2,1,0:T(8,128)(2,1)S(1)}, bf16[4,256,256]{2,1,0:T(8,128)(2,1)}, u32[]{:S(2)}) copy-start(bf16[4,256,256]{2,1,0:T(8,128)(2,1)} %constant.9.up_lo_ref) | copy-start | bytes 1572868
where the time goes:
time: 57.5 us; the launch traced here: 57.2 us
  blocking collectives  31.4 us (55%)
  Pallas kernels  11 us (19%)
  starting transfers between devices  9.49 us (17%)
  waiting for transfers between devices  5.3 us (9%)
    all_to_all x1, blocking collectives, local(): got = lax.all_to_all(packed, 'tmpl', 0, 0, tiled=True)  27.3 us
    ppermute x3, starting transfers between devices, moved(): lax.ppermute(own, 'tm', [(i, (i + by) % slots) for i in range(slots)])  9.49 us
    ppermute x3, waiting for transfers between devices, moved(): lax.ppermute(own, 'tm', [(i, (i + by) % slots) for i in range(slots)])  5.3 us
    pallas_call x1, Pallas kernels, call_filter(): pl.pallas_call(functools.partial(filter_and_rebuild, lambda: (*place(), s...  4.85 us
    all_gather x1, blocking collectives, local(): lax.all_gather(call_combine(got, weights, edge), 'band', axis=0, tiled=True)  4.07 us
    pallas_call x1, Pallas kernels, call_filter_two(): pl.pallas_call(functools.partial(filter_two, place), out_shape=pltpu.VMEM...  2.07 us
    pallas_call x1, Pallas kernels, call_filter_own(): pl.pallas_call(filter_own, out_shape=(half, half, pltpu.VMEM((tmpl, count...  1.95 us
    pallas_call x1, Pallas kernels, call_pack(): pl.pallas_call(functools.partial(pack_filters, place), out_shape=(pltpu.V...  1.43 us
  transfers between devices with their start and end apart: 3, of which 2 were waited for; matrix products, arithmetic and copies ran while one was open for 0% of the time, Pallas kernels for 7%

commit v1 on v0

--- a/solution.py
+++ b/solution.py
@@ -80,7 +80,7 @@
             value = jnp.where((lane >= at) & (lane < at + 32), turned[q - first][q : q + 1, :], value)
         line_ref[2 * rows + first // 4 : 2 * rows + first // 4 + 1, :] = value
     line_ref[2 * rows + 3 : 24, :] = jnp.zeros((24 - 2 * rows - 3, LANES), F32)
-    line = line_ref[...]
+    line = jnp.concatenate([line_ref[8 * k : 8 * k + 8, :] for k in range(3)], axis=1)
     for p in range(out_ref.shape[0]):
         out_ref[p] = line
     strain_ref[0:64, :] = shigh_ref[...]
@@ -99,11 +99,15 @@
     parts = got_ref.shape[0]
     basis = w_hi_ref.shape[1]
     rows = basis // parts
+
+    def row(k):
+        return got_ref[:, k % 8, LANES * (k // 8) : LANES * (k // 8 + 1)]
+
     for q in range(rows):
         at = pl.ds(q, parts, stride=rows)
         for t in range(2):
-            f_ref[t, at, :] = got_ref[:, rows * t + q, :]
-        low = got_ref[:, 2 * rows + q // 4, :]
+            f_ref[t, at, :] = row(rows * t + q)
+        low = row(2 * rows + q // 4)
         f_ref[2, at, :] = pltpu.roll(low, LANES - 32 * (q % 4), 1) if q % 4 else low
     taps = jnp.concatenate([f_ref[t] for t in range(2)], axis=1)
     h = dot3(w_hi_ref[...], w_lo_ref[...], *split(taps))
@@ -388,7 +392,7 @@
     return pl.pallas_call(
         functools.partial(pack_filters, place),
         out_shape=(
-            pltpu.VMEM((parts, 24, LANES), F32), half, half, half, half,
+            pltpu.VMEM((parts, 8, 3 * LANES), F32), half, half, half, half,
             pltpu.VMEM(strains[0].shape, F32), pltpu.VMEM((24, LANES), F32),
         ),
         in_specs=[SMEM] + [VMEM] * 9,

time: 57.5 us -> 57.4 us (level)
  no operation moved by 1% of the time
where the time goes in v1:
time: 57.4 us; the launch traced here: 57.1 us
  blocking collectives  31.4 us (55%)
  Pallas kernels  10.9 us (19%)
  starting transfers between devices  9.49 us (17%)
  waiting for transfers between devices  5.29 us (9%)
    all_to_all x1, blocking collectives, local(): got = lax.all_to_all(packed, 'tmpl', 0, 0, tiled=True)  27.3 us
    ppermute x3, starting transfers between devices, moved(): lax.ppermute(own, 'tm', [(i, (i + by) % slots) for i in range(slots)])  9.49 us
    ppermute x3, waiting for transfers between devices, moved(): lax.ppermute(own, 'tm', [(i, (i + by) % slots) for i in range(slots)])  5.29 us
    pallas_call x1, Pallas kernels, call_filter(): pl.pallas_call(functools.partial(filter_and_rebuild, lambda: (*place(), s...  4.85 us
    all_gather x1, blocking collectives, local(): lax.all_gather(call_combine(got, weights, edge), 'band', axis=0, tiled=True)  4.07 us
    pallas_call x1, Pallas kernels, call_filter_two(): pl.pallas_call(functools.partial(filter_two, place), out_shape=pltpu.VMEM...  2.07 us
    pallas_call x1, Pallas kernels, call_filter_own(): pl.pallas_call(filter_own, out_shape=(half, half, pltpu.VMEM((tmpl, count...  1.95 us
    pallas_call x1, Pallas kernels, call_pack(): pl.pallas_call(functools.partial(pack_filters, place), out_shape=(pltpu.V...  1.43 us
  transfers between devices with their start and end apart: 3, of which 2 were waited for; matrix products, arithmetic and copies ran while one was open for 0% of the time, Pallas kernels for 7%

profile of v1, /device:TPU:1, one launch (start us, length us, event | category | flops | bytes accessed | tf_op | source)
XLA Modules:
  0.0 57.1 jit_solution(9659015256023308964)
XLA Ops:
  0.0 1.4 %pack_filters.1 = (f32[32,8,384]{2,1,0:T(8,128)S(1)}, bf16[128,320]{1,0:T(8,128)(2,1)S(1)}, bf16[128,320]{1,0:T(8,128)(2,1)S(1)}, bf16[128,320]{1,0:T(8,128)(2,1...) custom-call(s32[3]{0:T(128)} %count_ref.1, f32[10,1024]{1,0:T(8,128)} %high_ref.1, ...), custom_call_target="tpu_custom_call" | custom-call | tf_op jit(solution)/shard_map/pack_filters/pallas_call | solution.py:392
  1.4 27.3 %all_to_all.5.got_ref = f32[32,8,384]{2,1,0:T(8,128)S(1)} all-to-all(f32[32,8,384]{2,1,0:T(8,128)S(1)} %get-tuple-element.15), channel_id=1, replica_groups=mesh['band'=2,'tmpl'=32,'tm'=8] {'tmpl'}, dimensions={0} | all-to-all | bytes 786432 | tf_op jit(solution)/shard_map/all_to_all | solution.py:509
  28.8 0.5 combine.1
  29.3 4.1 %all_gather.3.both_ref = f32[576,128]{1,0:T(8,128)S(1)} all-gather(f32[288,128]{1,0:T(8,128)S(1)} %combine.1), channel_id=1, replica_groups=mesh['band'=2,'tmpl'=32,'tm'=8] {'band'}, dimensions={0}, use_global_device_ids=true | all-gather | bytes 442368 | tf_op jit(solution)/shard_map/all_gather | solution.py:510
  33.4 0.1 select.1.own_ref
  33.4 5.1 %collective-permute-start.1 = (f32[296,128]{1,0:T(8,128)S(1)}, f32[296,128]{1,0:T(8,128)S(1)}, u32[]{:S(2)}, u32[]{:S(2)}) collective-permute-start(f32[296,128]{1,0:T(8,128)S(1)} %select.1.own_ref), channel_id=1, source_target_pairs={{0,7},{1,0},{2,1},{3,2},{4,3},{5,4},{6,5},{7,6},{8,15},{9,8},{10,9... | collective-permute-start | bytes 454664 | tf_op jit(solution)/shard_map/ppermute | solution.py:514
  38.5 1.9 %collective-permute-start.2 = (f32[296,128]{1,0:T(8,128)S(1)}, f32[296,128]{1,0:T(8,128)S(1)}, u32[]{:S(2)}, u32[]{:S(2)}) collective-permute-start(f32[296,128]{1,0:T(8,128)S(1)} %select.1.own_ref), channel_id=1, source_target_pairs={{0,2},{1,3},{2,4},{3,5},{4,6},{5,7},{6,0},{7,1},{8,10},{9,11},{10,... | collective-permute-start | bytes 454664 | tf_op jit(solution)/shard_map/ppermute | solution.py:514
  40.5 2.5 %collective-permute-start = (f32[296,128]{1,0:T(8,128)S(1)}, f32[296,128]{1,0:T(8,128)S(1)}, u32[]{:S(2)}, u32[]{:S(2)}) collective-permute-start(f32[296,128]{1,0:T(8,128)S(1)} %select.1.own_ref), channel_id=1, source_target_pairs={{0,1},{1,2},{2,3},{3,4},{4,5},{5,6},{6,7},{7,0},{8,9},{9,10},{10,1... | collective-permute-start | bytes 454664 | tf_op jit(solution)/shard_map/ppermute | solution.py:514
  43.0 2.0 %filter_own.1 = (bf16[128,9216]{1,0:T(8,128)(2,1)S(1)}, bf16[128,9216]{1,0:T(8,128)(2,1)S(1)}, f32[64,8960]{1,0:T(8,128)S(1)}) custom-call(f32[296,128]{1,0:T(8,128)S(1)} %select.1.own_ref, f32[64,128]{1,0:T(8,128)S(1)} %get-tuple-element.21.strain_ref), custom_call_target="tpu_custom_call" | custom-call | tf_op jit(solution)/shard_map/filter_own/pallas_call | solution.py:429
  44.9 0.0 collective-permute-done.1.right_ref
  44.9 5.2 %collective-permute-done.2.second_ref = f32[296,128]{1,0:T(8,128)S(1)} collective-permute-done((f32[296,128]{1,0:T(8,128)S(1)}, f32[296,128]{1,0:T(8,128)S(1)}, u32[]{:S(2)}, u32[]{:S(2)}) %collective-permute-start.2) | collective-permute-done | bytes 151584 | tf_op jit(solution)/shard_map/ppermute | solution.py:514
  50.1 0.0 copy-start
  50.1 0.0 copy-start.1
  50.1 2.1 %filter_two.1.part_ref = f32[64,8192]{1,0:T(8,128)S(1)} custom-call(f32[296,128]{1,0:T(8,128)S(1)} %collective-permute-done.1.right_ref, f32[296,128]{1,0:T(8,128)S(1)} %collective-permute-done.2.second_ref, bf16[128,9216]{1,0:T(8,128)(2,1)S(1)} %get-tuple-element.22.t_hi, bf16[128,9216]{1,0:T(8,128)(2,1)S(1)} %get-tuple-element.23.t_lo, ...), custom_call_target="tpu_custom_call" | custom-call | tf_op jit(solution)/shard_map/filter_two/pallas_call | solution.py:440
  52.2 0.1 collective-permute-done.left_ref
  52.3 0.0 copy-done
  52.3 0.0 copy-done.1
  52.3 4.8 %filter_and_rebuild.1 = f32[64,8192]{1,0:T(8,128)} custom-call(f32[296,128]{1,0:T(8,128)S(1)} %select.1.own_ref, f32[296,128]{1,0:T(8,128)S(1)} %collective-permute-done.left_ref, f32[296,128]{1,0:T(8,128)S(1)} %collective-permute-done.1.right_ref, f32[296,128]{1,0:T(8,128)S(1)} %collective-permute-done.2.second_ref, ...), custom_call_target="tpu_custom_call" | custom-call | tf_op jit(solution)/shard_map/filter_and_rebuild/pallas_call | solution.py:452
Async XLA Ops:
  33.4 11.5 %collective-permute-start.1 = (f32[296,128]{1,0:T(8,128)S(1)}, f32[296,128]{1,0:T(8,128)S(1)}, u32[]{:S(2)}, u32[]{:S(2)}) collective-permute-start(f32[296,128]{1,0:T(8,128)S(1)} %select.1.own_ref), channel_id=1, source_target_pairs={{0,7},{1,0},{2,1},{3,2},{4,3},{5,4},{6,5},{7,6},{8,15},{9,8},{10,9... | collective-permute-start | bytes 454664 | tf_op jit(solution)/shard_map/ppermute | solution.py:514
  38.5 11.6 %collective-permute-start.2 = (f32[296,128]{1,0:T(8,128)S(1)}, f32[296,128]{1,0:T(8,128)S(1)}, u32[]{:S(2)}, u32[]{:S(2)}) collective-permute-start(f32[296,128]{1,0:T(8,128)S(1)} %select.1.own_ref), channel_id=1, source_target_pairs={{0,2},{1,3},{2,4},{3,5},{4,6},{5,7},{6,0},{7,1},{8,10},{9,11},{10,... | collective-permute-start | bytes 454664 | tf_op jit(solution)/shard_map/ppermute | solution.py:514
  40.5 11.8 %collective-permute-start = (f32[296,128]{1,0:T(8,128)S(1)}, f32[296,128]{1,0:T(8,128)S(1)}, u32[]{:S(2)}, u32[]{:S(2)}) collective-permute-start(f32[296,128]{1,0:T(8,128)S(1)} %select.1.own_ref), channel_id=1, source_target_pairs={{0,1},{1,2},{2,3},{3,4},{4,5},{5,6},{6,7},{7,0},{8,9},{9,10},{10,1... | collective-permute-start | bytes 454664 | tf_op jit(solution)/shard_map/ppermute | solution.py:514
  50.1 2.2 %copy-start = (bf16[4,256,256]{2,1,0:T(8,128)(2,1)S(1)}, bf16[4,256,256]{2,1,0:T(8,128)(2,1)}, u32[]{:S(2)}) copy-start(bf16[4,256,256]{2,1,0:T(8,128)(2,1)} %constant.6.up_hi_ref) | copy-start | bytes 1572868
  50.1 2.2 %copy-start.1 = (bf16[4,256,256]{2,1,0:T(8,128)(2,1)S(1)}, bf16[4,256,256]{2,1,0:T(8,128)(2,1)}, u32[]{:S(2)}) copy-start(bf16[4,256,256]{2,1,0:T(8,128)(2,1)} %constant.9.up_lo_ref) | copy-start | bytes 1572868
